TPU v7x, 256 devices: a 8x8x2 block of a 8x8x16 slice. The times are simulated.
256 devices in a mesh: groups: 2 (over z), cells: 128 (over y, x, core).
Axes of the slice: x: 8, y: 8, z: 2, core: 2. Of those that a mesh axis runs over, the one named last changes fastest.
The devices are a block of a 8x8x16 slice.
Arguments:
- pair_act: bfloat16 [768, 384, 128], P(('groups', 'cells')), parts along dimension 0, may hold values from -6 to 6
- pair_mask: int32 [768, 384], P(('groups', 'cells')), parts along dimension 0, may hold values from 0 to 1, as said below
- chain_ids: int32 [768], P('groups'), parts along dimension 0, may hold values from 0 to 3, never falling along the last dimension, each value on 1 to 192 neighbouring positions
- proj_weight: bfloat16 [128, 256], replicated, may hold values from -0.5 to 0.5
- gate_weight: bfloat16 [128, 128], replicated, may hold values from -0.5 to 0.5
- chain_bias: float32 [2, 128], replicated, may hold values from -4 to 4
- out_weight: bfloat16 [64, 128], replicated, may hold values from -0.75 to 0.75
- out_grad: bfloat16 [768, 384, 128], P(('groups', 'cells')), parts along dimension 0, may hold values from -6 to 6
Outputs:
- pair_grad: bfloat16 [768, 384, 128], P(('groups', 'cells')), parts along dimension 0
- proj_weight_grad: float32 [256, 256], P('groups'), parts along dimension 0
- gate_weight_grad: float32 [256, 128], P('groups'), parts along dimension 0
- out_weight_grad: float32 [128, 128], P('groups'), parts along dimension 0
There are 2 independent parts, one for each index of `groups`. A program takes and returns all parts, laid end to end along the dimension named above; an argument that names none is the same for every part. Nothing has to cross between parts.
Inputs may be any that keep to these rules, and one draw needn't show every extreme that they name: pair_mask[i, j] = valid[i] * valid[j] for a 0 or 1 validity of each residue.
All inputs are finite; a program needn't handle non-finite values.
Results may differ from a plain program's by a relative error of at most 0.012.
Values may be sent and summed in bfloat16 or wider, within the bound.
A program may use at most 64 MiB of HBM per device.

v0:
```python
import jax
import jax.numpy as jnp
from jax import lax
from jax.sharding import PartitionSpec as P

EPS = 1e-05


def in_one(arrays, axis):
    ends = [0]
    for a in arrays:
        ends.append(ends[-1] + a.size)
    subtotal = lax.psum(jnp.concatenate([a.ravel() for a in arrays]), axis)
    return tuple((subtotal[b:e].reshape(a.shape) for a, b, e in zip(arrays, ends, ends[1:])))


def normalize_axis(values, axis):
    center = values - jnp.mean(values, axis=axis, keepdims=True)
    scale = lax.rsqrt(jnp.mean(center * center, axis=axis, keepdims=True) + EPS)
    return (center * scale, scale)


def norm_backward(grad, normed, scale, axis):
    first = jnp.mean(grad, axis=axis, keepdims=True)
    second = jnp.mean(grad * normed, axis=axis, keepdims=True)
    return scale * (grad - first - normed * second)


def local(
    pair_act, pair_mask, chain_ids, proj_weight, gate_weight, chain_bias, out_weight, out_grad
):
    devices = lax.axis_size("cells")
    rows_here = pair_act.shape[0]
    length = pair_act.shape[1]
    width = pair_act.shape[2]
    hidden = out_weight.shape[0]
    halfway = length // 2
    channel_pairs = devices // 2
    per_device = 2 * hidden // devices
    count = rows_here * length
    zfull = pair_act.astype(jnp.float32).reshape(count, width)
    zhat, zscale = normalize_axis(zfull, 1)
    normed = zhat.astype(jnp.bfloat16)
    projected = jnp.einsum("xc,cf->fx", normed, proj_weight, preferred_element_type=jnp.float32)
    keeper = pair_mask.astype(jnp.float32).reshape(1, count)
    values = projected[: 2 * hidden]
    sigma = jax.nn.sigmoid(projected[2 * hidden :])
    factors = (keeper * sigma * values).astype(jnp.bfloat16)
    outgoing = factors.reshape(2, channel_pairs, per_device, rows_here, 2, halfway)
    outgoing = jnp.transpose(outgoing, (1, 4, 0, 2, 3, 5)).reshape(
        devices, 2, per_device, rows_here, halfway
    )
    arrived = lax.all_to_all(outgoing, "cells", split_axis=0, concat_axis=3, tiled=True)
    left_half = arrived[0, 0]
    right_half = arrived[0, 1]
    partial_value = jnp.einsum(
        "cik,cjk->cij", left_half, right_half, preferred_element_type=jnp.float32
    )
    landed = lax.all_to_all(
        partial_value.reshape(per_device, devices, rows_here, length).astype(jnp.bfloat16),
        "cells",
        split_axis=1,
        concat_axis=0,
        tiled=True,
    ).astype(jnp.float32)
    landed = landed.reshape(channel_pairs, 2, per_device, rows_here, length)
    triangle = jnp.sum(landed, axis=1).reshape(hidden, count)
    tri_hat, tri_scale = normalize_axis(triangle, 0)
    tri_low = tri_hat.astype(jnp.bfloat16)
    outputs = jnp.einsum("hx,hc->xc", tri_low, out_weight, preferred_element_type=jnp.float32)
    start = lax.axis_index("cells") * rows_here
    own_chain = lax.dynamic_slice_in_dim(chain_ids, start, rows_here, 0)
    same_chain = (own_chain[:, None] == chain_ids[None, :]).reshape(count, 1)
    logits = jnp.dot(normed, gate_weight, preferred_element_type=jnp.float32)
    logits = logits + jnp.where(same_chain, chain_bias[0][None, :], chain_bias[1][None, :])
    gating = jax.nn.sigmoid(logits)
    upstream = out_grad.reshape(count, width).astype(jnp.float32)
    d_outputs = (upstream * gating).astype(jnp.bfloat16)
    d_logits = (upstream * outputs * gating * (1.0 - gating)).astype(jnp.bfloat16)
    out_term = jnp.einsum("hx,xc->hc", tri_low, d_outputs, preferred_element_type=jnp.float32)
    gate_term = jnp.einsum("xc,xd->cd", normed, d_logits, preferred_element_type=jnp.float32)
    d_hat = jnp.einsum("xc,hc->hx", d_outputs, out_weight, preferred_element_type=jnp.float32)
    d_tri = norm_backward(d_hat, tri_hat, tri_scale, 0).astype(jnp.bfloat16)
    doubled = jnp.broadcast_to(
        d_tri.reshape(channel_pairs, 1, per_device, rows_here, length),
        (channel_pairs, 2, per_device, rows_here, length),
    )
    whole = lax.all_to_all(
        doubled.reshape(devices, per_device, rows_here, length),
        "cells",
        split_axis=0,
        concat_axis=2,
        tiled=True,
    )[0]
    d_left = jnp.einsum("cij,cjk->cik", whole, right_half, preferred_element_type=jnp.float32)
    d_right = jnp.einsum("cij,cik->cjk", whole, left_half, preferred_element_type=jnp.float32)
    d_pair = jnp.stack([d_left, d_right]).astype(jnp.bfloat16)
    returned = lax.all_to_all(
        d_pair.reshape(2, per_device, devices, rows_here, halfway),
        "cells",
        split_axis=2,
        concat_axis=2,
        tiled=True,
    )
    returned = returned.reshape(2, per_device, channel_pairs, 2, rows_here, halfway)
    d_factors = (
        jnp.transpose(returned, (0, 2, 1, 4, 3, 5)).reshape(2 * hidden, count).astype(jnp.float32)
    )
    d_values = d_factors * keeper * sigma
    d_gates = d_factors * keeper * values * sigma * (1.0 - sigma)
    d_proj = jnp.concatenate([d_values, d_gates], axis=0).astype(jnp.bfloat16)
    proj_term = jnp.einsum("xc,fx->cf", normed, d_proj, preferred_element_type=jnp.float32)
    d_normed = jnp.einsum("fx,cf->xc", d_proj, proj_weight, preferred_element_type=jnp.float32)
    d_normed = d_normed + jnp.einsum(
        "xd,cd->xc", d_logits, gate_weight, preferred_element_type=jnp.float32
    )
    pair_grad = (
        norm_backward(d_normed, zhat, zscale, 1)
        .astype(jnp.bfloat16)
        .reshape(rows_here, length, width)
    )
    proj_sum, gate_sum, out_sum = in_one((proj_term, gate_term, out_term), "cells")
    factor = 1.0 / length
    return (pair_grad, proj_sum * factor, gate_sum * factor, out_sum * factor)


def solution(mesh):
    placed = (
        P(("groups", "cells"), None, None),
        P(("groups", "cells"), None),
        P("groups"),
        P(),
        P(),
        P(),
        P(),
        P(("groups", "cells"), None, None),
    )
    return jax.shard_map(
        local,
        mesh=mesh,
        in_specs=placed,
        out_specs=(
            P(("groups", "cells"), None, None),
            P("groups", None),
            P("groups", None),
            P("groups", None),
        ),
        check_vma=False,
    )
```

profile of v0, /device:TPU:513, one launch (start us, length us, event | category | flops | bytes accessed | tf_op | source)
XLA Modules:
  0.0 339.7 jit_solution(11828793296574214934)
XLA Ops:
  7.2 1.2 convert_reduce_fusion
  8.4 1.4 multiply_reduce_fusion.1
  9.8 0.7 convert_element_type.85
  10.5 1.3 fusion.15
  11.8 0.3 convolution_bitcast_fusion
  12.4 0.3 reshape.298
  12.7 1.1 copy.41
  13.8 27.4 %all-to-all-start = ((bf16[128,2,1,3,192]{4,1,3,2,0:T(2,128)(2,1)}), bf16[128,2,1,3,192]{4,1,3,2,0:T(2,128)(2,1)S(1)}, u32[]{:S(2)}, u32[]{:S(2)}) async-start(bf16[128,2,1,3,192]{4,1,3,2,0:T(2,128)(2,1)} %bitcast.4), calls=%async_computation | async-start | bytes 786432 | tf_op jit(solution)/shard_map/all_to_all | solution.py:53
  41.3 17.2 %all-to-all-done = bf16[128,2,1,3,192]{4,1,3,2,0:T(2,128)(2,1)S(1)} async-done(((bf16[128,2,1,3,192]{4,1,3,2,0:T(2,128)(2,1)}), bf16[128,2,1,3,192]{4,1,3,2,0:T(2,128)(2,1)S(1)}, u32[]{:S(2)}, u32[]{:S(2)}) %all-to-all-start) | async-done | bytes 294944 | tf_op jit(solution)/shard_map/all_to_all | solution.py:53
  58.5 1.5 fusion.38
  60.1 0.7 copy.57
  60.9 0.3 fusion.7
  61.2 1.0 copy.47
  62.2 7.6 %all-to-all-start.1 = ((bf16[1,128,3,384]{3,2,0,1:T(4,128)(2,1)}), bf16[1,128,3,384]{3,2,0,1:T(4,128)(2,1)S(1)}, u32[]{:S(2)}, u32[]{:S(2)}) async-start(bf16[1,128,3,384]{3,2,0,1:T(4,128)(2,1)} %copy.47), calls=%async_computation.1 | async-start | bytes 786432 | tf_op jit(solution)/shard_map/all_to_all | solution.py:59
  69.9 1.2 fusion.10
  71.1 15.6 %all-to-all-done.1 = bf16[1,128,3,384]{3,2,0,1:T(4,128)(2,1)S(1)} async-done(((bf16[1,128,3,384]{3,2,0,1:T(4,128)(2,1)}), bf16[1,128,3,384]{3,2,0,1:T(4,128)(2,1)S(1)}, u32[]{:S(2)}, u32[]{:S(2)}) %all-to-all-start.1) | async-done | bytes 294944 | tf_op jit(solution)/shard_map/all_to_all | solution.py:59
  86.7 0.2 convert_reduce_fusion.1
  86.9 0.3 reduce_sum.83
  87.4 0.3 fusion.23
  87.8 0.9 broadcast_in_dim.53
  88.6 7.4 %all-to-all-start.2 = ((bf16[128,1,3,384]{3,2,1,0:T(4,128)(2,1)}), bf16[128,1,3,384]{3,2,1,0:T(4,128)(2,1)S(1)}, u32[]{:S(2)}, u32[]{:S(2)}) async-start(bf16[128,1,3,384]{3,2,1,0:T(4,128)(2,1)} %bitcast.18), calls=%async_computation.2 | async-start | bytes 786432 | tf_op jit(solution)/shard_map/all_to_all | solution.py:88
  96.1 0.7 copy.56
  96.8 16.4 %all-to-all-done.2 = bf16[128,1,3,384]{3,2,1,0:T(4,128)(2,1)S(1)} async-done(((bf16[128,1,3,384]{3,2,1,0:T(4,128)(2,1)}), bf16[128,1,3,384]{3,2,1,0:T(4,128)(2,1)S(1)}, u32[]{:S(2)}, u32[]{:S(2)}) %all-to-all-start.2) | async-done | bytes 294944 | tf_op jit(solution)/shard_map/all_to_all | solution.py:88
  113.2 0.2 reshape.303
  113.4 0.2 copy.51
  113.8 0.3 fusion.9
  114.0 0.3 fusion.8
  114.4 1.2 copy.53
  115.6 7.4 %all-to-all-start.3 = ((bf16[2,1,128,3,192]{4,0,3,1,2:T(2,128)(2,1)}), bf16[2,1,128,3,192]{4,0,3,1,2:T(2,128)(2,1)S(1)}, u32[]{:S(2)}, u32[]{:S(2)}) async-start(bf16[2,1,128,3,192]{4,0,3,1,2:T(2,128)(2,1)} %copy.53), calls=%async_computation.3 | async-start | bytes 786432 | tf_op jit(solution)/shard_map/all_to_all | solution.py:98
  123.0 0.3 all-reduce.2.cloned.1.call-start
  123.5 1.4 fusion.6
  124.9 0.3 convolution_bitcast_fusion.1
  125.2 14.9 %all-to-all-done.3 = bf16[2,1,128,3,192]{4,0,3,1,2:T(2,128)(2,1)S(1)} async-done(((bf16[2,1,128,3,192]{4,0,3,1,2:T(2,128)(2,1)}), bf16[2,1,128,3,192]{4,0,3,1,2:T(2,128)(2,1)S(1)}, u32[]{:S(2)}, u32[]{:S(2)}) %all-to-all-start.3) | async-done | bytes 294944 | tf_op jit(solution)/shard_map/all_to_all | solution.py:98
  140.1 0.3 convert_bitcast_fusion
  140.4 0.4 copy.54
  140.8 0.6 reshape.312
  141.4 0.3 multiply_convert_fusion.2
  141.7 0.3 convolution_bitcast_fusion.2
  142.0 0.4 fusion.16
  142.4 0.2 copy-done.1
  142.6 0.7 fusion.37
  143.4 0.7 pad_maximum_fusion.4
  144.2 1.4 multiply_convert_fusion
  145.6 182.7 %all-reduce.2.cloned.1.call-done = f32[57344]{0:T(1024)} async-done(((f32[57344]{0:T(1024)}), f32[57344]{0:T(1024)}) %all-reduce.2.cloned.1.call-update) | async-done | bytes 229392 | tf_op jit(solution)/shard_map/psum | solution.py:13
  328.3 0.9 slice_multiply_fusion
  329.3 0.7 mul.168
  329.9 1.4 fusion.32
  331.3 1.5 fusion.31
  (47 shorter events, 1.3 us)
Async XLA Ops:
  7.2 4.6 %copy-start = (bf16[128,256]{1,0:T(8,128)(2,1)S(1)}, bf16[128,256]{1,0:T(8,128)(2,1)}, u32[]{:S(2)}) copy-start(bf16[128,256]{1,0:T(8,128)(2,1)} %param.11) | copy-start | bytes 196612
  12.4 28.9 %copy-start.8 = (s32[384]{0:T(512)S(1)}, s32[384]{0:T(512)}, u32[]{:S(2)}) copy-start(s32[384]{0:T(512)} %param.10) | copy-start | bytes 4612
  13.8 44.7 %all-to-all-start = ((bf16[128,2,1,3,192]{4,1,3,2,0:T(2,128)(2,1)}), bf16[128,2,1,3,192]{4,1,3,2,0:T(2,128)(2,1)S(1)}, u32[]{:S(2)}, u32[]{:S(2)}) async-start(bf16[128,2,1,3,192]{4,1,3,2,0:T(2,128)(2,1)} %bitcast.4), calls=%async_computation | async-start | bytes 786432 | tf_op jit(solution)/shard_map/all_to_all | solution.py:53
  60.8 9.1 %copy-start.9 = (f32[2,128]{1,0:T(2,128)S(1)}, f32[2,128]{1,0:T(2,128)}, u32[]{:S(2)}) copy-start(f32[2,128]{1,0:T(2,128)} %param.13) | copy-start | bytes 3076
  60.8 9.1 %copy-start.2 = (bf16[3,384,128]{2,1,0:T(8,128)(2,1)S(1)}, bf16[3,384,128]{2,1,0:T(8,128)(2,1)}, u32[]{:S(2)}) copy-start(bf16[3,384,128]{2,1,0:T(8,128)(2,1)} %param.15) | copy-start | bytes 884740
  60.8 9.1 %copy-start.6 = (bf16[128,128]{1,0:T(8,128)(2,1)S(1)}, bf16[128,128]{1,0:T(8,128)(2,1)}, u32[]{:S(2)}) copy-start(bf16[128,128]{1,0:T(8,128)(2,1)} %param.12) | copy-start | bytes 98308
  62.2 24.5 %all-to-all-start.1 = ((bf16[1,128,3,384]{3,2,0,1:T(4,128)(2,1)}), bf16[1,128,3,384]{3,2,0,1:T(4,128)(2,1)S(1)}, u32[]{:S(2)}, u32[]{:S(2)}) async-start(bf16[1,128,3,384]{3,2,0,1:T(4,128)(2,1)} %copy.47), calls=%async_computation.1 | async-start | bytes 786432 | tf_op jit(solution)/shard_map/all_to_all | solution.py:59
  71.1 16.3 %copy-start.4 = (bf16[64,128]{1,0:T(8,128)(2,1)S(1)}, bf16[64,128]{1,0:T(8,128)(2,1)}, u32[]{:S(2)}) copy-start(bf16[64,128]{1,0:T(8,128)(2,1)} %param.14) | copy-start | bytes 49156
  88.6 24.5 %all-to-all-start.2 = ((bf16[128,1,3,384]{3,2,1,0:T(4,128)(2,1)}), bf16[128,1,3,384]{3,2,1,0:T(4,128)(2,1)S(1)}, u32[]{:S(2)}, u32[]{:S(2)}) async-start(bf16[128,1,3,384]{3,2,1,0:T(4,128)(2,1)} %bitcast.18), calls=%async_computation.2 | async-start | bytes 786432 | tf_op jit(solution)/shard_map/all_to_all | solution.py:88
  114.4 9.1 %copy-start.3 = (bf16[3,384,128]{2,1,0:T(8,128)(2,1)S(1)}, bf16[3,384,128]{2,1,0:T(8,128)(2,1)}, u32[]{:S(2)}) copy-start(bf16[3,384,128]{2,1,0:T(8,128)(2,1)} %param.15) | copy-start | bytes 884740
  114.4 9.1 %copy-start.5 = (bf16[64,128]{1,0:T(8,128)(2,1)S(1)}, bf16[64,128]{1,0:T(8,128)(2,1)}, u32[]{:S(2)}) copy-start(bf16[64,128]{1,0:T(8,128)(2,1)} %param.14) | copy-start | bytes 49156
  115.6 24.5 %all-to-all-start.3 = ((bf16[2,1,128,3,192]{4,0,3,1,2:T(2,128)(2,1)}), bf16[2,1,128,3,192]{4,0,3,1,2:T(2,128)(2,1)S(1)}, u32[]{:S(2)}, u32[]{:S(2)}) async-start(bf16[2,1,128,3,192]{4,0,3,1,2:T(2,128)(2,1)} %copy.53), calls=%async_computation.3 | async-start | bytes 786432 | tf_op jit(solution)/shard_map/all_to_all | solution.py:98
  123.0 205.3 %all-reduce.2.cloned.1.call-start = ((), (), s32[]{:S(2)}) async-start(), calls=%async_computation.4 | async-start | bytes 458752 | tf_op jit(solution)/shard_map/psum | solution.py:13
  141.7 1.0 copy-start.1
  141.7 1.0 copy-start.7
Sparse Core Ops, SparseCore 0:
  144.3 183.9 all-reduce.1
where the time goes:
time: 340 us
  waiting for transfers between devices  247 us (73%)
  starting transfers between devices  50.2 us (15%)
  between operations  14.5 us (4%)
  other arithmetic  12 us (4%)
  local copies, waits for them, and re-layouts  10.4 us (3%)
  matrix products  5.81 us (2%)
    psum x1, waiting for transfers between devices, in_one(): subtotal = lax.psum(jnp.concatenate([a.ravel() for a in arrays]), axis)  183 us
    all_to_all x1, starting transfers between devices, local(): lax.all_to_all(outgoing, 'cells', split_axis=0, concat_axis=3, tiled=True)  27.4 us
    all_to_all x1, waiting for transfers between devices, local(): lax.all_to_all(outgoing, 'cells', split_axis=0, concat_axis=3, tiled=True)  17.2 us
    all_to_all x1, waiting for transfers between devices, local(): lax.all_to_all(doubled.reshape(devices, per_device, rows_here, length), '...  16.4 us
    all_to_all x1, waiting for transfers between devices, local(): lax.all_to_all(partial_value.reshape(per_device, devices, rows_here, leng...  15.6 us
    all_to_all x1, waiting for transfers between devices, local(): lax.all_to_all(d_pair.reshape(2, per_device, devices, rows_here, halfway)...  14.9 us
    all_to_all x1, starting transfers between devices, local(): lax.all_to_all(partial_value.reshape(per_device, devices, rows_here, leng...  7.62 us
    all_to_all x1, starting transfers between devices, local(): lax.all_to_all(d_pair.reshape(2, per_device, devices, rows_here, halfway)...  7.44 us
  transfers between devices with their start and end apart: 5, of which 5 were waited for; matrix products, arithmetic and copies ran while one was open for 2% of the time, Pallas kernels for 0%

commit v1 on v0

--- a/solution.py
+++ b/solution.py
@@ -10,7 +10,7 @@
     ends = [0]
     for a in arrays:
         ends.append(ends[-1] + a.size)
-    subtotal = lax.psum(jnp.concatenate([a.ravel() for a in arrays]), axis)
+    subtotal = jnp.sum(lax.all_gather(jnp.concatenate([a.ravel() for a in arrays]), axis), axis=0)
     return tuple((subtotal[b:e].reshape(a.shape) for a, b, e in zip(arrays, ends, ends[1:])))
 
 

time: 340 us -> 319 us (0.938)
  waiting for transfers between devices: 247 us -> 187 us
  local copies, waits for them, and re-layouts: 10.4 us -> 38.2 us
  other arithmetic: 12 us -> 21 us
    psum x1 -> x0, waiting for transfers between devices: 183 us -> none  [in_one(): subtotal = lax.psum(jnp.concatenate([a.ravel() for a in arrays]), axis)]
    all_gather x0 -> x1, waiting for transfers between devices: none -> 124 us  [in_one(): lax.all_gather(jnp.concatenate([a.ravel() for a in arrays]), axis)]
    all_gather x0 -> x1, local copies, waits for them, and re-layouts: none -> 26 us  [in_one(): lax.all_gather(jnp.concatenate([a.ravel() for a in arrays]), axis)]
    reduce_sum x0 -> x1, other arithmetic: none -> 10.9 us  [in_one(): jnp.sum(lax.all_gather(jnp.concatenate([a.ravel() for a in arrays]), axis...]
where the time goes in v1:
time: 319 us; the launch traced here: 318 us
  waiting for transfers between devices  187 us (59%)
  starting transfers between devices  50.4 us (16%)
  local copies, waits for them, and re-layouts  38.2 us (12%)
  other arithmetic  21 us (7%)
  between operations  14.5 us (5%)
  matrix products  6.44 us (2%)
    all_gather x1, waiting for transfers between devices, in_one(): lax.all_gather(jnp.concatenate([a.ravel() for a in arrays]), axis)  124 us
    all_to_all x1, starting transfers between devices, local(): lax.all_to_all(outgoing, 'cells', split_axis=0, concat_axis=3, tiled=True)  27.4 us
    all_gather x1, local copies, waits for them, and re-layouts, in_one(): lax.all_gather(jnp.concatenate([a.ravel() for a in arrays]), axis)  26 us
    all_to_all x1, waiting for transfers between devices, local(): lax.all_to_all(outgoing, 'cells', split_axis=0, concat_axis=3, tiled=True)  17.2 us
    all_to_all x1, waiting for transfers between devices, local(): lax.all_to_all(doubled.reshape(devices, per_device, rows_here, length), '...  16.4 us
    all_to_all x1, waiting for transfers between devices, local(): lax.all_to_all(partial_value.reshape(per_device, devices, rows_here, leng...  15.6 us
    all_to_all x1, waiting for transfers between devices, local(): lax.all_to_all(d_pair.reshape(2, per_device, devices, rows_here, halfway)...  14.3 us
    reduce_sum x1, other arithmetic, in_one(): jnp.sum(lax.all_gather(jnp.concatenate([a.ravel() for a in arrays]), axis...  10.9 us
  transfers between devices with their start and end apart: 5, of which 5 were waited for; matrix products, arithmetic and copies ran while one was open for 2% of the time, Pallas kernels for 0%

profile of v1, /device:TPU:513, one launch (start us, length us, event | category | flops | bytes accessed | tf_op | source)
XLA Modules:
  0.0 317.9 jit_solution(9246106325863713001)
XLA Ops:
  7.2 1.2 convert_reduce_fusion
  8.4 1.4 multiply_reduce_fusion.1
  9.8 0.7 convert_element_type.85
  10.5 1.3 fusion.15
  11.8 0.3 convolution_bitcast_fusion
  12.4 0.3 reshape.298
  12.7 1.1 copy.55
  13.8 27.4 %all-to-all-start = ((bf16[128,2,1,3,192]{4,1,3,2,0:T(2,128)(2,1)}), bf16[128,2,1,3,192]{4,1,3,2,0:T(2,128)(2,1)S(1)}, u32[]{:S(2)}, u32[]{:S(2)}) async-start(bf16[128,2,1,3,192]{4,1,3,2,0:T(2,128)(2,1)} %bitcast.4), calls=%async_computation | async-start | bytes 786432 | tf_op jit(solution)/shard_map/all_to_all | solution.py:53
  41.4 17.2 %all-to-all-done = bf16[128,2,1,3,192]{4,1,3,2,0:T(2,128)(2,1)S(1)} async-done(((bf16[128,2,1,3,192]{4,1,3,2,0:T(2,128)(2,1)}), bf16[128,2,1,3,192]{4,1,3,2,0:T(2,128)(2,1)S(1)}, u32[]{:S(2)}, u32[]{:S(2)}) %all-to-all-start) | async-done | bytes 294944 | tf_op jit(solution)/shard_map/all_to_all | solution.py:53
  58.6 1.5 fusion.38
  60.2 0.7 copy.71
  60.9 0.3 fusion.7
  61.2 1.0 copy.61
  62.2 7.6 %all-to-all-start.1 = ((bf16[1,128,3,384]{3,2,0,1:T(4,128)(2,1)}), bf16[1,128,3,384]{3,2,0,1:T(4,128)(2,1)S(1)}, u32[]{:S(2)}, u32[]{:S(2)}) async-start(bf16[1,128,3,384]{3,2,0,1:T(4,128)(2,1)} %copy.61), calls=%async_computation.1 | async-start | bytes 786432 | tf_op jit(solution)/shard_map/all_to_all | solution.py:59
  70.0 1.2 fusion.10
  71.1 15.6 %all-to-all-done.1 = bf16[1,128,3,384]{3,2,0,1:T(4,128)(2,1)S(1)} async-done(((bf16[1,128,3,384]{3,2,0,1:T(4,128)(2,1)}), bf16[1,128,3,384]{3,2,0,1:T(4,128)(2,1)S(1)}, u32[]{:S(2)}, u32[]{:S(2)}) %all-to-all-start.1) | async-done | bytes 294944 | tf_op jit(solution)/shard_map/all_to_all | solution.py:59
  87.0 0.3 reduce_sum.92
  87.4 0.3 fusion.23
  87.8 0.9 broadcast_in_dim.53
  88.7 7.4 %all-to-all-start.2 = ((bf16[128,1,3,384]{3,2,1,0:T(4,128)(2,1)}), bf16[128,1,3,384]{3,2,1,0:T(4,128)(2,1)S(1)}, u32[]{:S(2)}, u32[]{:S(2)}) async-start(bf16[128,1,3,384]{3,2,1,0:T(4,128)(2,1)} %bitcast.18), calls=%async_computation.2 | async-start | bytes 786432 | tf_op jit(solution)/shard_map/all_to_all | solution.py:88
  96.1 0.7 copy.70
  96.8 16.4 %all-to-all-done.2 = bf16[128,1,3,384]{3,2,1,0:T(4,128)(2,1)S(1)} async-done(((bf16[128,1,3,384]{3,2,1,0:T(4,128)(2,1)}), bf16[128,1,3,384]{3,2,1,0:T(4,128)(2,1)S(1)}, u32[]{:S(2)}, u32[]{:S(2)}) %all-to-all-start.2) | async-done | bytes 294944 | tf_op jit(solution)/shard_map/all_to_all | solution.py:88
  113.4 0.9 copy.65
  114.3 1.1 reshape.304
  115.4 0.3 fusion.9
  115.7 0.3 fusion.8
  116.0 1.2 copy.67
  117.2 7.6 %all-to-all-start.3 = ((bf16[2,1,128,3,192]{4,0,3,1,2:T(2,128)(2,1)}), bf16[2,1,128,3,192]{4,0,3,1,2:T(2,128)(2,1)S(1)}, u32[]{:S(2)}, u32[]{:S(2)}) async-start(bf16[2,1,128,3,192]{4,0,3,1,2:T(2,128)(2,1)} %copy.67), calls=%async_computation.3 | async-start | bytes 786432 | tf_op jit(solution)/shard_map/all_to_all | solution.py:98
  124.8 0.3 all-gather.3.cloned.1.call-start
  125.3 1.4 fusion.6
  126.7 0.9 convolution_bitcast_fusion.1
  127.6 14.3 %all-to-all-done.3 = bf16[2,1,128,3,192]{4,0,3,1,2:T(2,128)(2,1)S(1)} async-done(((bf16[2,1,128,3,192]{4,0,3,1,2:T(2,128)(2,1)}), bf16[2,1,128,3,192]{4,0,3,1,2:T(2,128)(2,1)S(1)}, u32[]{:S(2)}, u32[]{:S(2)}) %all-to-all-start.3) | async-done | bytes 294944 | tf_op jit(solution)/shard_map/all_to_all | solution.py:98
  141.8 0.3 convert_bitcast_fusion
  142.1 0.4 copy.68
  142.5 0.6 reshape.312
  143.2 0.9 multiply_convert_fusion.2
  144.1 0.3 convolution_bitcast_fusion.2
  144.6 0.4 copy-done.5
  144.9 0.7 pad_maximum_fusion.4
  145.7 0.4 fusion.16
  146.1 0.7 fusion.37
  146.9 1.4 multiply_convert_fusion
  148.2 123.9 %all-gather.3.cloned.1.call-done = f32[7340032]{0:T(1024)} async-done(((f32[57344]{0:T(1024)}), f32[7340032]{0:T(1024)}) %all-gather.3.cloned.1.call-update) | async-done | bytes 29360144 | tf_op jit(solution)/shard_map/all_gather | solution.py:13
  272.1 26.0 %reshape.314 = f32[128,57344]{1,0:T(8,128)} reshape(f32[7340032]{0:T(1024)} %all-gather.3.cloned.1.call-done) | data formatting | bytes 58720256 | tf_op jit(solution)/shard_map/all_gather | solution.py:13
  298.1 10.9 %reduce_sum.99 = f32[57344]{0:T(1024)S(1)} reduce(f32[128,57344]{1,0:T(8,128)} %reshape.314, f32[]{:T(128)} %constant.10.clone.1), dimensions={0}, to_apply=%region_9.10 | reduce | flops 7282688 | bytes 29589508 | tf_op jit(solution)/shard_map/reduce_sum | solution.py:13
  309.1 0.6 fusion.31
  309.7 0.6 fusion.32
  310.3 0.7 mul.168
  (53 shorter events, 1.6 us)
Async XLA Ops:
  7.2 4.7 %copy-start = (bf16[128,256]{1,0:T(8,128)(2,1)S(1)}, bf16[128,256]{1,0:T(8,128)(2,1)}, u32[]{:S(2)}) copy-start(bf16[128,256]{1,0:T(8,128)(2,1)} %param.11) | copy-start | bytes 196612
  10.5 1.7 copy-start.6
  12.4 28.9 %copy-start.10 = (s32[384]{0:T(512)S(1)}, s32[384]{0:T(512)}, u32[]{:S(2)}) copy-start(s32[384]{0:T(512)} %param.10) | copy-start | bytes 4612
  13.8 44.7 %all-to-all-start = ((bf16[128,2,1,3,192]{4,1,3,2,0:T(2,128)(2,1)}), bf16[128,2,1,3,192]{4,1,3,2,0:T(2,128)(2,1)S(1)}, u32[]{:S(2)}, u32[]{:S(2)}) async-start(bf16[128,2,1,3,192]{4,1,3,2,0:T(2,128)(2,1)} %bitcast.4), calls=%async_computation | async-start | bytes 786432 | tf_op jit(solution)/shard_map/all_to_all | solution.py:53
  60.9 9.0 %copy-start.11 = (f32[2,128]{1,0:T(2,128)S(1)}, f32[2,128]{1,0:T(2,128)}, u32[]{:S(2)}) copy-start(f32[2,128]{1,0:T(2,128)} %param.13) | copy-start | bytes 3076
  60.9 9.0 %copy-start.3 = (bf16[3,384,128]{2,1,0:T(8,128)(2,1)S(1)}, bf16[3,384,128]{2,1,0:T(8,128)(2,1)}, u32[]{:S(2)}) copy-start(bf16[3,384,128]{2,1,0:T(8,128)(2,1)} %param.15) | copy-start | bytes 884740
  60.9 9.0 %copy-start.8 = (bf16[128,128]{1,0:T(8,128)(2,1)S(1)}, bf16[128,128]{1,0:T(8,128)(2,1)}, u32[]{:S(2)}) copy-start(bf16[128,128]{1,0:T(8,128)(2,1)} %param.12) | copy-start | bytes 98308
  62.2 24.5 %all-to-all-start.1 = ((bf16[1,128,3,384]{3,2,0,1:T(4,128)(2,1)}), bf16[1,128,3,384]{3,2,0,1:T(4,128)(2,1)S(1)}, u32[]{:S(2)}, u32[]{:S(2)}) async-start(bf16[1,128,3,384]{3,2,0,1:T(4,128)(2,1)} %copy.61), calls=%async_computation.1 | async-start | bytes 786432 | tf_op jit(solution)/shard_map/all_to_all | solution.py:59
  71.1 16.3 %copy-start.7 = (bf16[64,128]{1,0:T(8,128)(2,1)S(1)}, bf16[64,128]{1,0:T(8,128)(2,1)}, u32[]{:S(2)}) copy-start(bf16[64,128]{1,0:T(8,128)(2,1)} %param.14) | copy-start | bytes 49156
  88.7 24.5 %all-to-all-start.2 = ((bf16[128,1,3,384]{3,2,1,0:T(4,128)(2,1)}), bf16[128,1,3,384]{3,2,1,0:T(4,128)(2,1)S(1)}, u32[]{:S(2)}, u32[]{:S(2)}) async-start(bf16[128,1,3,384]{3,2,1,0:T(4,128)(2,1)} %bitcast.18), calls=%async_computation.2 | async-start | bytes 786432 | tf_op jit(solution)/shard_map/all_to_all | solution.py:88
  117.2 8.1 %copy-start.4 = (bf16[3,384,128]{2,1,0:T(8,128)(2,1)S(1)}, bf16[3,384,128]{2,1,0:T(8,128)(2,1)}, u32[]{:S(2)}) copy-start(bf16[3,384,128]{2,1,0:T(8,128)(2,1)} %param.15) | copy-start | bytes 884740
  117.2 24.6 %all-to-all-start.3 = ((bf16[2,1,128,3,192]{4,0,3,1,2:T(2,128)(2,1)}), bf16[2,1,128,3,192]{4,0,3,1,2:T(2,128)(2,1)S(1)}, u32[]{:S(2)}, u32[]{:S(2)}) async-start(bf16[2,1,128,3,192]{4,0,3,1,2:T(2,128)(2,1)} %copy.67), calls=%async_computation.3 | async-start | bytes 786432 | tf_op jit(solution)/shard_map/all_to_all | solution.py:98
  124.8 147.3 %all-gather.3.cloned.1.call-start = ((), (), s32[]{:S(2)}) async-start(), calls=%async_computation.4 | async-start | bytes 29589504 | tf_op jit(solution)/shard_map/all_gather | solution.py:13
  144.1 0.8 copy-start.5
  144.5 1.6 copy-start.2
  144.5 1.6 copy-start.9
  298.1 12.9 %copy-start.1 = (bf16[128,256]{1,0:T(8,128)(2,1)S(1)}, bf16[128,256]{1,0:T(8,128)(2,1)}, u32[]{:S(2)}) copy-start(bf16[128,256]{1,0:T(8,128)(2,1)} %param.11) | copy-start | bytes 196612
Sparse Core Ops, SparseCore 0:
  145.8 126.2 all-gather.2
